TPU v7x, 128 devices: a whole 4x4x4 slice. The times are simulated.
128 devices in a mesh: trial: 32 (over z, y, core), geno: 4 (over x).
Axes of the slice: x: 4, y: 4, z: 4, core: 2. Of those that a mesh axis runs over, the one named last changes fastest.
Arguments:
- probe_signs: int32 [16, 128, 1, 44, 256], P(None, ('trial', 'geno')), may hold values 0 or 1
- trial_rows: int32 [32], P('trial'), may hold values from 89 to 176
- trial_cols: int32 [32], P('trial'), may hold values from 128 to 256
- ar_rho: float32 [32, 2], P('trial'), may hold values from 0.1 to 0.7
- res_var: float32 [32], P('trial'), may hold values from 4 to 16
- plot_owner: int32 [128, 1, 44, 256, 1], P(('trial', 'geno')), may hold values from 0 to 127; in each aligned block of 11264 rows (0 to 11263, 11264 to 22527, ..., all dimensions but the last counted through in order) at most 176 rows name the same one
- plot_slot: int32 [128, 1, 44, 256], P(('trial', 'geno')), may hold values from 0 to 1023
Outputs:
- geno_terms: float32 [3, 16, 131072], P(None, None, ('trial', 'geno'))
Inputs may be any that keep to these rules, and one draw needn't show every extreme that they name: `plot_owner`: among the plot positions of one device at most 176 name the same owner, and in every draw some device has exactly 176 positions for one owner. A plot's genotype is 1024 * plot_owner + plot_slot.
All inputs are finite; a program needn't handle non-finite values. No bound on the sum of `probe_signs` on one device may be relied on, other than what follows from the above.
Results may differ from a plain program's by a relative error of at most 0.0028.
Values may be sent and summed in bfloat16 or wider, within the bound.
A program may use at most 64 MiB of HBM per device.

v0:
```python
import math

import jax
import jax.numpy as jnp
from jax import lax
from jax.sharding import PartitionSpec as P

G_DEV = 1024


def extended_2(block, sides, width):
    for axis, dim in sides:
        count = lax.axis_size(axis)
        forward = [(i, i + 1) for i in range(count - 1)]
        backward = [(target, source) for source, target in forward]
        low = lax.ppermute(
            lax.slice_in_dim(block, block.shape[dim] - width, None, axis=dim), axis, forward
        )
        high = lax.ppermute(lax.slice_in_dim(block, 0, width, axis=dim), axis, backward)
        block = jnp.concatenate([low, block, high], axis=dim)
    return block


def line_coeffs(rho_vals, cell_count, positions):
    inverse = 1.0 / (1.0 - rho_vals * rho_vals)
    edge_mask = (positions[None, :] == 0) | (positions[None, :] == cell_count[:, None] - 1)
    inside = 1.0 + rho_vals * rho_vals
    main_diag = jnp.where(edge_mask, inverse[:, None], (inverse * inside)[:, None])
    main_slope = jnp.where(
        edge_mask,
        (2.0 * rho_vals * inverse * inverse)[:, None],
        (4.0 * rho_vals * inverse * inverse)[:, None],
    )
    off_diag = -inverse * rho_vals
    off_slope = -inside * inverse * inverse
    return (main_diag, off_diag, main_slope, off_slope)


def across_columns(field_vals, main_diag, off_diag):
    padded = jnp.pad(field_vals, ((0, 0), (0, 0), (0, 0), (1, 1)))
    return main_diag[:, None, :] * field_vals + off_diag[:, None, None] * (
        padded[..., :-2] + padded[..., 2:]
    )


def across_rows(padded, main_diag, off_diag):
    return main_diag[:, :, None] * padded[:, :, 1:-1, :] + off_diag[:, None, None] * (
        padded[:, :, :-2, :] + padded[:, :, 2:, :]
    )


def body(probe_signs, trial_rows, trial_cols, ar_rho, res_var, plot_owner, plot_slot):
    sign_bits = probe_signs[:, 0]
    probe_count, tile_count, row_count, col_count = sign_bits.shape
    band_index = lax.axis_index("geno")
    row_pos = band_index * row_count + jnp.arange(row_count, dtype=jnp.int32)
    col_pos = jnp.arange(col_count, dtype=jnp.int32)
    present = (row_pos[None, :, None] < trial_rows[:, None, None]) & (
        col_pos[None, None, :] < trial_cols[:, None, None]
    )
    probe_field = jnp.where(
        present[None], 2.0 * sign_bits.astype(jnp.float32) - 1.0, jnp.float32(0.0)
    )
    edge_rows = jnp.stack([probe_field[:, :, 0, :], probe_field[:, :, -1, :]], 0).astype(
        jnp.bfloat16
    )
    rim_rows = extended_2(edge_rows, (("geno", 0),), 1)
    extended = jnp.concatenate(
        [
            rim_rows[0][:, :, None, :].astype(jnp.float32),
            probe_field,
            rim_rows[3][:, :, None, :].astype(jnp.float32),
        ],
        axis=2,
    )
    col_diag, col_off, col_sdiag, col_soff = line_coeffs(ar_rho[:, 1], trial_cols, col_pos)
    row_diag, row_off, row_sdiag, row_soff = line_coeffs(ar_rho[:, 0], trial_rows, row_pos)
    col_field = across_columns(extended, col_diag, col_off)
    col_slope = across_columns(extended, col_sdiag, col_soff)
    plot_scale = jnp.where(present, (1.0 / res_var)[:, None, None], jnp.float32(0.0))
    plot_terms = jnp.stack(
        [
            across_rows(col_field, row_diag, row_off) * plot_scale[None],
            across_rows(col_field, row_sdiag, row_soff) * plot_scale[None],
            across_rows(col_slope, row_diag, row_off) * plot_scale[None],
        ],
        0,
    ).astype(jnp.bfloat16)
    term_rows = 3 * probe_count
    plot_count = tile_count * row_count * col_count
    term_flat = plot_terms.reshape(term_rows, plot_count)
    owners = plot_owner.reshape(plot_count)
    slot_code = plot_slot.reshape(plot_count) + 1
    slot_rows = jnp.stack([slot_code // 64, slot_code % 64], 0).astype(jnp.bfloat16)
    payload = jnp.concatenate([term_flat, slot_rows], 0)
    payload_rows = term_rows + 2
    trial_size = lax.axis_size("trial")
    geno_size = lax.axis_size("geno")
    devices = trial_size * geno_size
    capacity = max(2, 2 * plot_count // devices)
    width = devices * capacity
    block = math.gcd(plot_count, 512)
    parts = math.gcd(width, 8)
    part_width = width // parts
    device_ids = jnp.arange(devices, dtype=jnp.int32)
    block_pos = jnp.arange(block, dtype=jnp.int32)
    lower = (block_pos[:, None] > block_pos[None, :]).astype(jnp.bfloat16)
    part_cols = jnp.arange(part_width, dtype=jnp.int32)

    def pack_block(step, carry):
        running, packed = carry
        start = step * block
        owner_block = lax.dynamic_slice_in_dim(owners, start, block, 0)
        pay_block = lax.dynamic_slice_in_dim(payload, start, block, 1)
        owner_hot = owner_block[:, None] == device_ids[None, :]
        before = jnp.dot(lower, owner_hot.astype(jnp.bfloat16), preferred_element_type=jnp.float32)
        place = jnp.sum(
            jnp.where(owner_hot, before + running[None, :], jnp.float32(0.0)), axis=1
        ).astype(jnp.int32)
        dest = owner_block * capacity + place
        for part in range(parts):
            select = (dest[:, None] == part * part_width + part_cols[None, :]).astype(jnp.bfloat16)
            packed = packed.at[:, part * part_width : (part + 1) * part_width].add(
                jnp.dot(pay_block, select, preferred_element_type=jnp.float32)
            )
        running = running + jnp.sum(owner_hot.astype(jnp.float32), axis=0)
        return (running, packed)

    start_carry = (
        jnp.zeros((devices,), jnp.float32),
        jnp.zeros((payload_rows, width), jnp.float32),
    )
    packed = lax.fori_loop(0, plot_count // block, pack_block, start_carry)[1].astype(jnp.bfloat16)
    got_values = lax.all_to_all(
        packed.reshape(payload_rows, devices, capacity),
        ("trial", "geno"),
        split_axis=1,
        concat_axis=1,
        tiled=True,
    )
    got_values = got_values.reshape(payload_rows, width)
    got_terms = got_values[:term_rows]
    got_code = got_values[term_rows].astype(jnp.float32) * 64.0 + got_values[term_rows + 1].astype(
        jnp.float32
    )
    got_slots = got_code.astype(jnp.int32) - 1
    block_rows = math.gcd(width, 1024)
    genotypes = jnp.arange(G_DEV, dtype=jnp.int32)

    def add_block(block_step, total):
        block_start = block_step * block_rows
        value_block = lax.dynamic_slice_in_dim(got_terms, block_start, block_rows, 1)
        slot_block = lax.dynamic_slice_in_dim(got_slots, block_start, block_rows, 0)
        incidence = (slot_block[:, None] == genotypes[None, :]).astype(jnp.bfloat16)
        return total + jnp.dot(value_block, incidence, preferred_element_type=jnp.float32)

    geno_sums = lax.fori_loop(
        0, width // block_rows, add_block, jnp.zeros((term_rows, G_DEV), jnp.float32)
    )
    return geno_sums.reshape(3, probe_count, G_DEV)


def solution(mesh):
    return jax.shard_map(
        body,
        mesh=mesh,
        in_specs=(
            P(None, ("trial", "geno"), None, None, None),
            P("trial"),
            P("trial"),
            P("trial", None),
            P("trial"),
            P(("trial", "geno"), None, None, None, None),
            P(("trial", "geno"), None, None, None),
        ),
        out_specs=P(None, None, ("trial", "geno")),
        check_vma=False,
    )
```

profile of v0, /device:TPU:1, one launch (start us, length us, event | category | flops | bytes accessed | tf_op | source)
XLA Modules:
  0.0 877.0 jit_solution(15543997992897450074)
XLA Ops:
  4.1 4.6 collective-permute-start
  28.6 719.4 %while.44 = (s32[]{:T(128)}, f32[128]{0:T(128)S(1)}, f32[50,22528]{1,0:T(8,128)}, s32[11264]{0:T(1024)}, bf16[50,11264]{1,0:T(8,128)(2,1)S(1)}, /*index=5*/pred[...) while((s32[]{:T(128)}, f32[128]{0:T(128)S(1)}, ...), condition=%wide.region_11.12_spmd.clone.clone, body=%wide.region_7.11_spmd.clone.clone.sunk | while | flops 1235399040 | bytes 10756342 | solution.py:133
  31.2 3.8 fusion.201
  35.1 3.8 fusion.202
  57.5 3.8 fusion.208
  63.9 3.8 fusion.201
  67.8 3.8 fusion.202
  90.2 3.8 fusion.208
  96.6 3.8 fusion.201
  100.5 3.8 fusion.202
  122.9 3.8 fusion.208
  129.3 3.8 fusion.201
  133.2 3.8 fusion.202
  155.6 3.8 fusion.208
  162.0 3.8 fusion.201
  165.9 3.8 fusion.202
  188.3 3.8 fusion.208
  194.7 3.8 fusion.201
  198.6 3.8 fusion.202
  221.0 3.8 fusion.208
  227.4 3.8 fusion.201
  231.3 3.8 fusion.202
  253.7 3.8 fusion.208
  260.1 3.8 fusion.201
  264.0 3.8 fusion.202
  286.4 3.8 fusion.208
  292.8 3.8 fusion.201
  296.7 3.8 fusion.202
  319.1 3.8 fusion.208
  325.5 3.8 fusion.201
  329.4 3.8 fusion.202
  351.8 3.8 fusion.208
  358.2 3.8 fusion.201
  362.1 3.8 fusion.202
  384.5 3.8 fusion.208
  390.9 3.8 fusion.201
  394.8 3.8 fusion.202
  417.2 3.8 fusion.208
  423.6 3.8 fusion.201
  427.5 3.8 fusion.202
  449.9 3.8 fusion.208
  456.3 3.8 fusion.201
  460.2 3.8 fusion.202
  482.6 3.8 fusion.208
  489.0 3.8 fusion.201
  492.9 3.8 fusion.202
  515.3 3.8 fusion.208
  521.7 3.8 fusion.201
  525.6 3.8 fusion.202
  554.4 3.8 fusion.201
  580.7 3.8 fusion.208
  587.1 3.8 fusion.201
  619.8 3.8 fusion.201
  652.5 3.8 fusion.201
  656.4 3.8 fusion.202
  678.8 3.8 fusion.208
  685.2 3.8 fusion.201
  717.9 3.8 fusion.201
  748.0 4.2 convert_element_type.177
  752.1 7.3 reshape.950
  763.2 11.9 %all-to-all-start = ((bf16[50,128,176]{2,0,1:T(8,128)(2,1)}), bf16[50,128,176]{2,0,1:T(8,128)(2,1)}, u32[]{:S(2)}, u32[]{:S(2)}) async-start(bf16[50,128,176]{2,0,1:T(8,128)(2,1)} %copy.19), calls=%async_computation | async-start | bytes 7340032 | tf_op jit(solution)/shard_map/all_to_all | solution.py:134
  775.1 47.3 %all-to-all-done = bf16[50,128,176]{2,0,1:T(8,128)(2,1)} async-done(((bf16[50,128,176]{2,0,1:T(8,128)(2,1)}), bf16[50,128,176]{2,0,1:T(8,128)(2,1)}, u32[]{:S(2)}, u32[]{:S(2)}) %all-to-all-start) | async-done | bytes 2252832 | tf_op jit(solution)/shard_map/all_to_all | solution.py:134
  827.6 6.7 slice.368
  834.2 42.0 %while.43 = (s32[]{:T(128)}, f32[48,1024]{1,0:T(8,128)S(1)}, bf16[48,22528]{1,0:T(8,128)(2,1)}, s32[22528]{0:T(1024)S(1)}, s32[]{:T(128)}, /*index=5*/s32[]{:T(128)}, s32[]{:T(128)}, s32[]{:T(128)}) while((s32[]{:T(128)}, f32[48,1024]{1,0:T(8,128)S(1)}, bf16[48,22528]{1,0:T(8,128)(2,1)}, s32[22528]{0:T(1024)S(1)}, s32[]{:T(128)}, ...), condition=%wide.region_13.14_spmd.clone, body=%wide.region_12.13_spmd.clone.sunk | while | flops 101810184 | bytes 503957 | solution.py:157
  (498 shorter events, 571.6 us)
Async XLA Ops:
  0.0 17.1 %copy-start = (s32[1,1,44,256]{3,1,2,0:T(1,128)S(1)}, s32[1,1,44,256]{3,1,2,0:T(1,128)}, u32[]{:S(2)}) copy-start(s32[1,1,44,256]{3,1,2,0:T(1,128)} %param.33) | copy-start | bytes 135172
  2.8 20.8 %collective-permute-start.1 = (bf16[1,16,1,256]{3,1,2,0:T(8,128)(2,1)S(1)}, bf16[1,16,1,256]{3,1,2,0:T(8,128)(2,1)S(1)}, u32[]{:S(2)}, u32[]{:S(2)}) collective-permute-start(bf16[1,16,1,256]{3,1,2,0:T(8,128)(2,1)S(1)} %get-tuple-element.784), channel_id=1, source_target_pairs={{1,0},{2,1},{3,2},{5,4},{6,5},{7,6},{9,8},{10,9},{11,10},{13,12},{... | collective-permute-start | bytes 24584 | tf_op jit(solution)/shard_map/ppermute | solution.py:19
  4.1 19.5 %collective-permute-start = (bf16[1,16,1,256]{3,1,2,0:T(8,128)(2,1)S(1)}, bf16[1,16,1,256]{3,1,2,0:T(8,128)(2,1)S(1)}, u32[]{:S(2)}, u32[]{:S(2)}) collective-permute-start(bf16[1,16,1,256]{3,1,2,0:T(8,128)(2,1)S(1)} %get-tuple-element.783), channel_id=1, source_target_pairs={{0,1},{1,2},{2,3},{4,5},{5,6},{6,7},{8,9},{9,10},{10,11},{12,13},{... | collective-permute-start | bytes 24584 | tf_op jit(solution)/shard_map/ppermute | solution.py:16
  763.2 59.2 %all-to-all-start = ((bf16[50,128,176]{2,0,1:T(8,128)(2,1)}), bf16[50,128,176]{2,0,1:T(8,128)(2,1)}, u32[]{:S(2)}, u32[]{:S(2)}) async-start(bf16[50,128,176]{2,0,1:T(8,128)(2,1)} %copy.19), calls=%async_computation | async-start | bytes 7340032 | tf_op jit(solution)/shard_map/all_to_all | solution.py:134
  876.3 0.7 copy-start.1
where the time goes:
time: 889 us; the launch traced here: 877 us
  matrix products  708 us (80%)
  other arithmetic  48.8 us (5%)
  waiting for transfers between devices  47.3 us (5%)
  local copies, waits for them, and re-layouts  45.1 us (5%)
  starting transfers between devices  17.7 us (2%)
    dot_general x176, matrix products, pack_block(): jnp.dot(pay_block, select, preferred_element_type=jnp.float32)  660 us
    all_to_all x1, waiting for transfers between devices, body(): lax.all_to_all(packed.reshape(payload_rows, devices, capacity), ('trial',...  47.3 us
    dot_general x22, matrix products, add_block(): jnp.dot(value_block, incidence, preferred_element_type=jnp.float32)  41 us
    another operation x32, other arithmetic  21.1 us
  transfers between devices with their start and end apart: 3, of which 1 were waited for; matrix products, arithmetic and copies ran while one was open for 1% of the time, Pallas kernels for 0%

commit v1 on v0

v1 whole, which is shorter than its diff:
```python
import functools

import jax
import jax.numpy as jnp
from jax import lax
from jax.experimental import pallas as pl
from jax.experimental.pallas import tpu as pltpu
from jax.sharding import PartitionSpec as P

G_DEV = 1024
PROBES = 16
FR = 44
FC = 256
DEVICES = 128
PER_ROW = 5
WORDS = 24
SLOTS = 176
ROWS = 36
PAD_ROWS = 40
BATCH = 16
BATCHES = DEVICES // BATCH
STEP = 37
SCALE_BITS = 24
MESH = pl.DeviceIdType.MESH
F32 = jnp.float32
BF16 = jnp.bfloat16
I32 = jnp.int32


def shifted(k):
    trial, geno = lax.axis_index("trial"), lax.axis_index("geno")
    core = lax.rem(lax.rem(trial, 2) + k // 64, 2)
    y = lax.rem(lax.rem(trial // 2, 4) + lax.rem(k // 4, 4), 4)
    z = lax.rem(trial // 8 + lax.rem(k // 16, 4), 4)
    x = lax.rem(geno + lax.rem(k, 4), 4)
    return z * 8 + y * 2 + core, x


def kernel(
    signs_ref, rows_ref, cols_ref, rho_ref, var_ref, owner_ref, slot_ref, out_ref,
    xs, us, vs, halo, table, picks, picks_s, sbuf, rbuf, digits, acc,
    in_sem, pick_sem, halo_send, halo_recv, send_sem, recv_sem,
):
    trial, geno = lax.axis_index("trial"), lax.axis_index("geno")
    barrier = pltpu.get_barrier_semaphore()

    loads = [
        pltpu.make_async_copy(signs_ref.at[p], xs.at[:, p, :], in_sem.at[p]) for p in range(PROBES)
    ]
    for load in loads:
        load.start()

    def greet(k, carry):
        pl.semaphore_signal(barrier, inc=1, device_id=shifted(k), device_id_type=MESH)
        return carry

    lax.fori_loop(1, DEVICES, greet, 0)

    owner_id = lax.broadcasted_iota(I32, (DEVICES, FC), 0)
    col_i = lax.broadcasted_iota(I32, (FC, FC), 0)
    col_j = lax.broadcasted_iota(I32, (FC, FC), 1)
    upto = jnp.where(col_i <= col_j, F32(1), F32(0)).astype(BF16)
    place_id = lax.broadcasted_iota(I32, (SLOTS, FC), 0)
    col_f = lax.broadcasted_iota(I32, (1, FC), 1).astype(F32)
    digits[...] = jnp.zeros_like(digits)

    def rank_row(r, running):
        own = owner_id == owner_ref[pl.ds(r, 1), :]
        hot = jnp.where(own, F32(1), F32(0)).astype(BF16)
        count = jnp.dot(hot, upto, preferred_element_type=F32) + running
        place = jnp.sum(jnp.where(own, count, F32(0)), axis=0, keepdims=True) - 1.0
        at_place = place_id == place.astype(I32)
        row_no = (r + 1).astype(F32)
        carry_row = jnp.where(at_place, row_no, F32(0))
        carry_col = jnp.where(at_place, col_f, F32(0))
        both = jnp.concatenate([carry_row, carry_col], axis=0).astype(BF16)
        digits[...] += lax.dot_general(
            hot, both, (((1,), (1,)), ((), ())), preferred_element_type=F32
        )
        return jnp.broadcast_to(count[:, FC - 1 :], (DEVICES, FC))

    def rank_rows(q, running):
        for i in range(4):
            running = rank_row(q * 4 + i, running)
        return running

    lax.fori_loop(0, FR // 4, rank_rows, jnp.zeros((DEVICES, FC), F32))
    chosen = (digits[:, :SLOTS] * float(FC) + digits[:, SLOTS:]).astype(I32)
    picks[:, :SLOTS] = jnp.clip(chosen, 0, (FR + 1) * FC - 1)
    picks[:, SLOTS:] = jnp.zeros((DEVICES, FC - SLOTS), I32)
    to_smem = pltpu.make_async_copy(picks, picks_s, pick_sem)
    to_smem.start()

    n_rows, n_cols = rows_ref[0], cols_ref[0]
    rho_r = jnp.full((1, FC), rho_ref[0, 0], F32)
    rho_c = jnp.full((1, FC), rho_ref[0, 1], F32)
    res = jnp.full((1, FC), var_ref[0], F32)
    col = lax.broadcasted_iota(I32, (1, FC), 1)

    def line(rho):
        inv = 1.0 / (1.0 - rho * rho)
        inside = 1.0 + rho * rho
        return (
            (inv, inv * inside, -inv * rho),
            (2.0 * rho * inv * inv, 4.0 * rho * inv * inv, -inside * inv * inv),
        )

    (ce, ci, co), (cse, csi, cso) = line(rho_c)
    (re, ri, ro), (rse, rsi, rso) = line(rho_r)
    col_edge = (col == 0) | (col == n_cols - 1)
    cd = jnp.where(col_edge, ce, ci)
    csd = jnp.where(col_edge, cse, csi)
    in_col = col < n_cols
    left_ok = col > 0
    right_ok = col < FC - 1
    inv_res = 1.0 / res
    c_top = jnp.maximum(ce, ci) - 2.0 * co
    cs_top = jnp.maximum(cse, csi) - 2.0 * cso
    r_top = jnp.maximum(re, ri) - 2.0 * ro
    rs_top = jnp.maximum(rse, rsi) - 2.0 * rso
    tops = [r_top * c_top * inv_res, rs_top * c_top * inv_res, r_top * cs_top * inv_res]
    scale_ints = [jnp.ceil(top * float(1 << SCALE_BITS)).astype(I32) + 1 for top in tops]
    gains = [
        inv_res * 32766.0 / (s.astype(F32) * (1.0 / float(1 << SCALE_BITS))) for s in scale_ints
    ]
    sub8 = lax.broadcasted_iota(I32, (8, FC), 0)
    scale_rows = jnp.where(
        sub8 == 5, scale_ints[0], jnp.where(sub8 == 6, scale_ints[1], scale_ints[2])
    )

    lane = lax.broadcasted_iota(I32, (1, 128), 1)
    group = jnp.where(lane < PER_ROW * WORDS, lane // WORDS, lane - PER_ROW * WORDS)
    group = jnp.where(group >= PER_ROW, 0, group)
    masks = [group == j for j in range(PER_ROW)]
    lane8 = lax.broadcasted_iota(I32, (8, 128), 1)
    first_scales = jnp.where(
        lane8 == 125, scale_ints[0][:, :128],
        jnp.where(lane8 == 126, scale_ints[1][:, :128], scale_ints[2][:, :128]),
    )
    table[0:8, :] = jnp.where(lane8 >= 125, first_scales, jnp.where(lane8 >= 120, -1, 0))

    for load in loads:
        load.wait()

    def columns(bits, row):
        present = in_col & (row >= 0) & (row < n_rows)
        p = jnp.where(present, 2.0 * bits.astype(F32) - 1.0, F32(0))
        beside = jnp.where(left_ok, pltpu.roll(p, 1, 1), F32(0)) + jnp.where(
            right_ok, pltpu.roll(p, FC - 1, 1), F32(0)
        )
        return cd * p + co * beside, csd * p + cso * beside

    def columns_row(r, carry):
        u, v = columns(xs[r], geno * FR + r)
        us[r + 1] = u
        vs[r + 1] = v
        return carry

    lax.fori_loop(0, FR, columns_row, 0)

    def terms_row(r, carry):
        row = geno * FR + r
        edge = (row == 0) | (row == n_rows - 1)
        rd = jnp.where(edge, re, ri)
        rsd = jnp.where(edge, rse, rsi)
        present = in_col & (row < n_rows)
        k0, k1, k2 = [jnp.where(present, gain, F32(0)) for gain in gains]
        u, v = us[r + 1], vs[r + 1]
        u2 = us[r] + us[r + 2]
        v2 = vs[r] + vs[r + 2]
        values = [
            (rd * u + ro * u2) * k0,
            (rsd * u + rso * u2) * k1,
            (rd * v + ro * v2) * k2,
        ]
        words = []
        for value in values:
            q = jnp.floor(value + 0.5).astype(I32)
            words.append((q[8:] << 16) | (q[:8] & 0xFFFF))
        aux = jnp.where(sub8 < PER_ROW, slot_ref[pl.ds(r, 1), :], scale_rows)
        stacked = jnp.concatenate(words * PER_ROW + [aux], axis=0)
        table[pl.ds(pl.multiple_of((r + 1) * FC, FC), FC), :] = stacked.T
        return carry

    lax.fori_loop(1, FR - 1, terms_row, 0)

    pl.semaphore_wait(barrier, DEVICES - 1)
    above = (trial, lax.rem(geno + 3, 4))
    below = (trial, lax.rem(geno + 1, 4))
    edges = [
        pltpu.make_async_remote_copy(
            src_ref=xs.at[0], dst_ref=halo.at[1], send_sem=halo_send.at[0],
            recv_sem=halo_recv.at[1], device_id=above, device_id_type=MESH,
        ),
        pltpu.make_async_remote_copy(
            src_ref=xs.at[FR - 1], dst_ref=halo.at[0], send_sem=halo_send.at[1],
            recv_sem=halo_recv.at[0], device_id=below, device_id_type=MESH,
        ),
    ]
    for edge in edges:
        edge.start()
    for edge in edges:
        edge.wait()
    for side, r in ((0, -1), (1, FR)):
        row = jnp.where((geno == 0) & (side == 0), -1, geno * FR + r)
        u, v = columns(halo[side], row)
        us[r + 1] = u
        vs[r + 1] = v
    lax.fori_loop(0, 2, lambda i, carry: terms_row(i * (FR - 1), carry), 0)
    to_smem.wait()

    def gather(target, dst):
        for r in range(ROWS):
            row = None
            for j in range(PER_ROW):
                slot = min(r * PER_ROW + j, FC - 1)
                part = table[pl.ds(picks_s[target, slot], 1), :]
                row = part if row is None else jnp.where(masks[j], part, row)
            dst[pl.ds(r, 1), :] = row

    def copy_of(s):
        k = lax.rem(s * STEP, DEVICES)
        t, g = shifted(k)
        return pltpu.make_async_remote_copy(
            src_ref=sbuf.at[s], dst_ref=rbuf.at[s, pl.ds(0, ROWS)],
            send_sem=send_sem.at[s], recv_sem=recv_sem.at[s],
            device_id=(t, g), device_id_type=MESH,
        )

    gather(trial * 4 + geno, rbuf.at[0])
    acc[...] = jnp.zeros_like(acc)

    def fill(s, carry):
        t, g = shifted(lax.rem(s * STEP, DEVICES))
        gather(t * 4 + g, sbuf.at[s])

        @pl.when(s > 1)
        def _():
            copy_of(s - 1).start()

        return carry

    width = BATCH * PAD_ROWS
    high_id = lax.broadcasted_iota(I32, (FC, width), 0)
    pos = lax.rem(lax.broadcasted_iota(I32, (1, width), 1), PAD_ROWS)

    def add_batch(b):
        def arrive(s, carry):
            copy_of(s).wait_recv()
            return carry

        lax.fori_loop(jnp.maximum(b * BATCH, 1), (b + 1) * BATCH, arrive, 0)
        block = rbuf[pl.ds(b * BATCH, BATCH)].reshape(width, 128).T
        scales = [
            block[125 + t : 126 + t, :].astype(F32) * (1.0 / (float(1 << SCALE_BITS) * 32766.0))
            for t in range(3)
        ]
        total = acc[...]
        for j in range(PER_ROW):
            slot = jnp.where(pos < ROWS, block[120 + j : 121 + j, :], -1)
            low = slot >> 8
            hot = jnp.where(high_id == (slot & 255), F32(1), F32(0)).astype(BF16)
            parts = []
            for t in range(3):
                word = block[(j * 3 + t) * 8 : (j * 3 + t + 1) * 8, :]
                parts.append(((word << 16) >> 16).astype(F32) * scales[t])
                parts.append((word >> 16).astype(F32) * scales[t])
            values = jnp.concatenate(parts, axis=0)
            split = jnp.concatenate(
                [jnp.where(low == q, values, F32(0)) for q in range(4)], axis=0
            ).astype(BF16)
            total = total + lax.dot_general(
                split, hot, (((1,), (1,)), ((), ())), preferred_element_type=F32
            )
        acc[...] = total

    def stage(b, carry):
        lax.fori_loop(jnp.maximum(b * BATCH, 1), (b + 1) * BATCH, fill, 0)

        @pl.when(b >= 2)
        def _():
            add_batch(b - 2)

        return carry

    lax.fori_loop(0, BATCHES, stage, 0)
    copy_of(DEVICES - 1).start()
    add_batch(BATCHES - 2)
    add_batch(BATCHES - 1)
    for q in range(4):
        out_ref[:, q * FC : (q + 1) * FC] = acc[q * 48 : (q + 1) * 48, :]

    def sent(s, carry):
        copy_of(s).wait_send()
        return carry

    lax.fori_loop(1, DEVICES, sent, 0)


def body(probe_signs, trial_rows, trial_cols, ar_rho, res_var, plot_owner, plot_slot):
    smem = pl.BlockSpec(memory_space=pltpu.SMEM)
    vmem = pl.BlockSpec(memory_space=pltpu.VMEM)
    out = pl.pallas_call(
        kernel,
        out_shape=jax.ShapeDtypeStruct((3 * PROBES, G_DEV), F32),
        in_specs=[pl.BlockSpec(memory_space=pl.ANY), smem, smem, smem, smem, vmem, vmem],
        out_specs=vmem,
        scratch_shapes=[
            pltpu.VMEM((FR, PROBES, FC), I32),
            pltpu.VMEM((FR + 2, PROBES, FC), F32),
            pltpu.VMEM((FR + 2, PROBES, FC), F32),
            pltpu.VMEM((2, PROBES, FC), I32),
            pltpu.VMEM(((FR + 1) * FC, 128), I32),
            pltpu.VMEM((DEVICES, FC), I32),
            pltpu.SMEM((DEVICES, FC), I32),
            pltpu.VMEM((DEVICES, ROWS, 128), I32),
            pltpu.VMEM((DEVICES, PAD_ROWS, 128), I32),
            pltpu.VMEM((DEVICES, 2 * SLOTS), F32),
            pltpu.VMEM((12 * PROBES, FC), F32),
            pltpu.SemaphoreType.DMA((PROBES,)),
            pltpu.SemaphoreType.DMA,
            pltpu.SemaphoreType.DMA((2,)),
            pltpu.SemaphoreType.DMA((2,)),
            pltpu.SemaphoreType.DMA((DEVICES,)),
            pltpu.SemaphoreType.DMA((DEVICES,)),
        ],
        compiler_params=pltpu.CompilerParams(
            collective_id=0, has_side_effects=True, vmem_limit_bytes=56 << 20
        ),
        name="hutchinson_exchange",
    )(
        probe_signs.reshape(PROBES, FR, FC),
        trial_rows,
        trial_cols,
        ar_rho,
        res_var,
        plot_owner.reshape(FR, FC),
        plot_slot.reshape(FR, FC),
    )
    return out.reshape(3, PROBES, G_DEV)


def solution(mesh):
    return jax.shard_map(
        body,
        mesh=mesh,
        in_specs=(
            P(None, ("trial", "geno"), None, None, None),
            P("trial"),
            P("trial"),
            P("trial", None),
            P("trial"),
            P(("trial", "geno"), None, None, None, None),
            P(("trial", "geno"), None, None, None),
        ),
        out_specs=P(None, None, ("trial", "geno")),
        check_vma=False,
    )
```

time: 889 us -> 91.9 us (0.10); the launches traced: 877 us -> 91.6 us
  matrix products: 708 us -> 0 us
  Pallas kernels: 0 us -> 83.9 us
  other arithmetic: 48.8 us -> 0 us
  waiting for transfers between devices: 47.3 us -> 0 us
  local copies, waits for them, and re-layouts: 45.1 us -> 5.76 us
  starting transfers between devices: 17.7 us -> 0 us
    dot_general x220 -> x0, matrix products: 708 us -> none  [the longest x176 660 us: pack_block(): jnp.dot(pay_block, select, preferred_element_type=jnp.float32)]
    pallas_call x0 -> x1, Pallas kernels: none -> 83.9 us  [body(): pl.pallas_call(kernel, out_shape=jax.ShapeDtypeStruct((3 * PROBES, G_DEV)...]
    all_to_all x1 -> x0, waiting for transfers between devices: 47.3 us -> none  [body(): lax.all_to_all(packed.reshape(payload_rows, devices, capacity), ('trial',...]
    another operation x34 -> x0, other arithmetic: 21.7 us -> none
    add x200 -> x0, other arithmetic: 18.7 us -> none  [the longest x22 16.9 us: pack_block(): dest = owner_block * capacity + place]
    dynamic_slice x44 -> x0, local copies, waits for them, and re-layouts: 16.9 us -> none  [the longest x22 16.7 us: pack_block(): owner_block = lax.dynamic_slice_in_dim(owners, start, block, 0)]
    slice x5 -> x0, local copies, waits for them, and re-layouts: 12.6 us -> none  [the longest x3 9.87 us: body(): got_terms = got_values[:term_rows]]
    all_to_all x1 -> x0, starting transfers between devices: 11.9 us -> none  [body(): lax.all_to_all(packed.reshape(payload_rows, devices, capacity), ('trial',...]
  transfers between devices with their start and end apart: 3 -> 0, of which waited for: 1 -> 0; matrix products, arithmetic and copies ran while one was open for 1% -> 0% of each run, Pallas kernels for 0% -> 0%
where the time goes in v1:
time: 91.9 us; the launch traced here: 91.6 us
  Pallas kernels  83.9 us (91%)
  local copies, waits for them, and re-layouts  5.76 us (6%)
  between operations  1.96 us (2%)
    pallas_call x1, Pallas kernels, body(): pl.pallas_call(kernel, out_shape=jax.ShapeDtypeStruct((3 * PROBES, G_DEV)...  83.9 us
    unnamed x5, local copies, waits for them, and re-layouts  3.68 us
    reshape x1, local copies, waits for them, and re-layouts, body(): probe_signs.reshape(PROBES, FR, FC)  2.08 us

profile of v1, /device:TPU:1, one launch (start us, length us, event | category | flops | bytes accessed | tf_op | source)
XLA Modules:
  0.0 91.6 jit_solution(15313682144663569538)
XLA Ops:
  1.9 0.0 copy-start
  2.0 1.4 %copy.18 = s32[1,1,44,256,1]{3,2,4,1,0:T(8,128)} copy(s32[1,1,44,256,1]{3,4,2,1,0:T(1,128)} %param.12) | data formatting | bytes 90112
  3.4 0.0 copy-done
  3.4 0.6 copy.17
  4.0 2.1 %copy.16 = s32[16,1,1,44,256]{4,3,0,1,2:T(8,128)} copy(s32[16,1,1,44,256]{4,2,3,1,0:T(1,128)} %param.7) | data formatting | bytes 1441792 | tf_op jit(solution)/shard_map/reshape | solution.py:332
  6.1 83.9 %hutchinson_exchange.1 = f32[48,1024]{1,0:T(8,128)} custom-call(s32[16,44,256]{2,1,0:T(8,128)} %bitcast.11, s32[1]{0:T(128)S(6)} %copy.20.rows_ref, s32[1]{0:T(128)S(6)} %copy.21.cols_ref, f32[1,2]{1,0:T(1,128)} %rho_ref.1, f32[1]{0:T(128)S(6)} %copy.22.var_ref, s32[44,256]{1,0:T(8,128)} %bitcast.13, s32[44,256]{1,0:T(8,128)} %bitcast.14), custom_call_target="tpu_custom_call" | custom-call | tf_op jit(solution)/shard_map/hutchinson_exchange/pallas_call | solution.py:303
  90.0 1.6 %copy.23 = f32[3,16,1024]{2,1,0:T(8,128)} copy(f32[3,16,1024]{2,1,0:T(8,128)} %bitcast.12) | data formatting | bytes 393216
Async XLA Ops:
  1.9 1.4 %copy-start = (s32[1,1,44,256]{3,1,2,0:T(1,128)S(1)}, s32[1,1,44,256]{3,1,2,0:T(1,128)}, u32[]{:S(2)}) copy-start(s32[1,1,44,256]{3,1,2,0:T(1,128)} %param.13) | copy-start | bytes 135172

commit v2 on v1

--- a/solution.py
+++ b/solution.py
@@ -1,5 +1,3 @@
-import functools
-
 import jax
 import jax.numpy as jnp
 from jax import lax
@@ -19,7 +17,8 @@
 PAD_ROWS = 40
 BATCH = 16
 BATCHES = DEVICES // BATCH
-STEP = 37
+RANK_ROWS = 4
+TERM_ROWS = 3
 SCALE_BITS = 24
 MESH = pl.DeviceIdType.MESH
 F32 = jnp.float32
@@ -27,13 +26,19 @@
 I32 = jnp.int32
 
 
-def shifted(k):
+def places():
     trial, geno = lax.axis_index("trial"), lax.axis_index("geno")
-    core = lax.rem(lax.rem(trial, 2) + k // 64, 2)
-    y = lax.rem(lax.rem(trial // 2, 4) + lax.rem(k // 4, 4), 4)
-    z = lax.rem(trial // 8 + lax.rem(k // 16, 4), 4)
-    x = lax.rem(geno + lax.rem(k, 4), 4)
-    return z * 8 + y * 2 + core, x
+    return trial // 8, lax.rem(trial // 2, 4), lax.rem(trial, 2), geno
+
+
+def shifted(step, i):
+    z, y, core, x = places()
+    far = step // 4
+    near = lax.rem(step, 4)
+    tz = lax.rem(z + lax.rem(far, 4) + 2 * near + i, 4)
+    ty = lax.rem(y + near, 4)
+    tc = lax.rem(core + far // 4 + near + i // 2, 2)
+    return tz * 8 + ty * 2 + tc, lax.rem(x + i, 4)
 
 
 def kernel(
@@ -45,16 +50,23 @@
     barrier = pltpu.get_barrier_semaphore()
 
     loads = [
-        pltpu.make_async_copy(signs_ref.at[p], xs.at[:, p, :], in_sem.at[p]) for p in range(PROBES)
+        pltpu.make_async_copy(signs_ref.at[p, :, 0], xs.at[:, p, :], in_sem.at[p])
+        for p in range(PROBES)
     ]
     for load in loads:
         load.start()
 
-    def greet(k, carry):
-        pl.semaphore_signal(barrier, inc=1, device_id=shifted(k), device_id_type=MESH)
-        return carry
-
-    lax.fori_loop(1, DEVICES, greet, 0)
+    def signal(step, i):
+        pl.semaphore_signal(barrier, inc=1, device_id=shifted(step, i), device_id_type=MESH)
+
+    def greet(step, carry):
+        for i in range(4):
+            signal(step, i)
+        return carry
+
+    for i in range(1, 4):
+        signal(0, i)
+    lax.fori_loop(1, DEVICES // 4, greet, 0)
 
     owner_id = lax.broadcasted_iota(I32, (DEVICES, FC), 0)
     col_i = lax.broadcasted_iota(I32, (FC, FC), 0)
@@ -64,30 +76,31 @@
     col_f = lax.broadcasted_iota(I32, (1, FC), 1).astype(F32)
     digits[...] = jnp.zeros_like(digits)
 
-    def rank_row(r, running):
-        own = owner_id == owner_ref[pl.ds(r, 1), :]
-        hot = jnp.where(own, F32(1), F32(0)).astype(BF16)
-        count = jnp.dot(hot, upto, preferred_element_type=F32) + running
-        place = jnp.sum(jnp.where(own, count, F32(0)), axis=0, keepdims=True) - 1.0
-        at_place = place_id == place.astype(I32)
-        row_no = (r + 1).astype(F32)
-        carry_row = jnp.where(at_place, row_no, F32(0))
-        carry_col = jnp.where(at_place, col_f, F32(0))
-        both = jnp.concatenate([carry_row, carry_col], axis=0).astype(BF16)
+    def rank_rows(q, running):
+        lefts, rights = [], []
+        for i in range(RANK_ROWS):
+            r = q * RANK_ROWS + i
+            own = owner_id == owner_ref[r]
+            hot = jnp.where(own, F32(1), F32(0)).astype(BF16)
+            count = jnp.dot(hot, upto, preferred_element_type=F32) + running
+            running = jnp.broadcast_to(count[:, FC - 1 :], (DEVICES, FC))
+            place = jnp.sum(jnp.where(own, count, F32(0)), axis=0, keepdims=True) - 1.0
+            lefts.append(jnp.where(place_id == place.astype(I32), F32(1), F32(0)).astype(BF16))
+            row_no = (r + 1).astype(F32)
+            rights.append(
+                jnp.concatenate(
+                    [jnp.where(own, row_no, F32(0)), jnp.where(own, col_f, F32(0))], axis=0
+                ).astype(BF16)
+            )
         digits[...] += lax.dot_general(
-            hot, both, (((1,), (1,)), ((), ())), preferred_element_type=F32
+            jnp.concatenate(lefts, axis=1), jnp.concatenate(rights, axis=1),
+            (((1,), (1,)), ((), ())), preferred_element_type=F32,
         )
-        return jnp.broadcast_to(count[:, FC - 1 :], (DEVICES, FC))
-
-    def rank_rows(q, running):
-        for i in range(4):
-            running = rank_row(q * 4 + i, running)
         return running
 
-    lax.fori_loop(0, FR // 4, rank_rows, jnp.zeros((DEVICES, FC), F32))
-    chosen = (digits[:, :SLOTS] * float(FC) + digits[:, SLOTS:]).astype(I32)
-    picks[:, :SLOTS] = jnp.clip(chosen, 0, (FR + 1) * FC - 1)
-    picks[:, SLOTS:] = jnp.zeros((DEVICES, FC - SLOTS), I32)
+    lax.fori_loop(0, FR // RANK_ROWS, rank_rows, jnp.zeros((DEVICES, FC), F32))
+    plot = (digits[:, :DEVICES] * float(FC) + digits[:, DEVICES:]).astype(I32)
+    picks[...] = jnp.clip(plot, 0, (FR + 1) * FC - 1)
     to_smem = pltpu.make_async_copy(picks, picks_s, pick_sem)
     to_smem.start()
 
@@ -150,15 +163,33 @@
         )
         return cd * p + co * beside, csd * p + cso * beside
 
-    def columns_row(r, carry):
-        u, v = columns(xs[r], geno * FR + r)
-        us[r + 1] = u
-        vs[r + 1] = v
-        return carry
-
-    lax.fori_loop(0, FR, columns_row, 0)
-
-    def terms_row(r, carry):
+    def columns_rows(q, carry):
+        for i in range(4):
+            r = q * 4 + i
+            u, v = columns(xs[r], geno * FR + r)
+            us[r + 1] = u
+            vs[r + 1] = v
+        return carry
+
+    lax.fori_loop(0, FR // 4, columns_rows, 0)
+
+    pl.semaphore_wait(barrier, DEVICES - 1)
+    above = (trial, lax.rem(geno + 3, 4))
+    below = (trial, lax.rem(geno + 1, 4))
+    edges = [
+        pltpu.make_async_remote_copy(
+            src_ref=xs.at[0], dst_ref=halo.at[1], send_sem=halo_send.at[0],
+            recv_sem=halo_recv.at[1], device_id=above, device_id_type=MESH,
+        ),
+        pltpu.make_async_remote_copy(
+            src_ref=xs.at[FR - 1], dst_ref=halo.at[0], send_sem=halo_send.at[1],
+            recv_sem=halo_recv.at[0], device_id=below, device_id_type=MESH,
+        ),
+    ]
+    for edge in edges:
+        edge.start()
+
+    def terms_row(r):
         row = geno * FR + r
         edge = (row == 0) | (row == n_rows - 1)
         rd = jnp.where(edge, re, ri)
@@ -177,28 +208,16 @@
         for value in values:
             q = jnp.floor(value + 0.5).astype(I32)
             words.append((q[8:] << 16) | (q[:8] & 0xFFFF))
-        aux = jnp.where(sub8 < PER_ROW, slot_ref[pl.ds(r, 1), :], scale_rows)
+        aux = jnp.where(sub8 < PER_ROW, slot_ref[r], scale_rows)
         stacked = jnp.concatenate(words * PER_ROW + [aux], axis=0)
         table[pl.ds(pl.multiple_of((r + 1) * FC, FC), FC), :] = stacked.T
-        return carry
-
-    lax.fori_loop(1, FR - 1, terms_row, 0)
-
-    pl.semaphore_wait(barrier, DEVICES - 1)
-    above = (trial, lax.rem(geno + 3, 4))
-    below = (trial, lax.rem(geno + 1, 4))
-    edges = [
-        pltpu.make_async_remote_copy(
-            src_ref=xs.at[0], dst_ref=halo.at[1], send_sem=halo_send.at[0],
-            recv_sem=halo_recv.at[1], device_id=above, device_id_type=MESH,
-        ),
-        pltpu.make_async_remote_copy(
-            src_ref=xs.at[FR - 1], dst_ref=halo.at[0], send_sem=halo_send.at[1],
-            recv_sem=halo_recv.at[0], device_id=below, device_id_type=MESH,
-        ),
-    ]
-    for edge in edges:
-        edge.start()
+
+    def inner_rows(q, carry):
+        for i in range(TERM_ROWS):
+            terms_row(1 + q * TERM_ROWS + i)
+        return carry
+
+    lax.fori_loop(0, (FR - 2) // TERM_ROWS, inner_rows, 0)
     for edge in edges:
         edge.wait()
     for side, r in ((0, -1), (1, FR)):
@@ -206,39 +225,49 @@
         u, v = columns(halo[side], row)
         us[r + 1] = u
         vs[r + 1] = v
-    lax.fori_loop(0, 2, lambda i, carry: terms_row(i * (FR - 1), carry), 0)
+
+    def outer_row(i, carry):
+        terms_row(i * (FR - 1))
+        return carry
+
+    lax.fori_loop(0, 2, outer_row, 0)
     to_smem.wait()
 
     def gather(target, dst):
         for r in range(ROWS):
             row = None
             for j in range(PER_ROW):
-                slot = min(r * PER_ROW + j, FC - 1)
-                part = table[pl.ds(picks_s[target, slot], 1), :]
+                place = min(r * PER_ROW + j, SLOTS - 1)
+                part = table[pl.ds(picks_s.at[place][target], 1), :]
+                if r * PER_ROW + j >= SLOTS:
+                    part = table[0:1, :]
                 row = part if row is None else jnp.where(masks[j], part, row)
             dst[pl.ds(r, 1), :] = row
 
-    def copy_of(s):
-        k = lax.rem(s * STEP, DEVICES)
-        t, g = shifted(k)
+    def copy_of(s, target=None):
         return pltpu.make_async_remote_copy(
             src_ref=sbuf.at[s], dst_ref=rbuf.at[s, pl.ds(0, ROWS)],
             send_sem=send_sem.at[s], recv_sem=recv_sem.at[s],
-            device_id=(t, g), device_id_type=MESH,
+            device_id=below if target is None else target, device_id_type=MESH,
         )
 
-    gather(trial * 4 + geno, rbuf.at[0])
     acc[...] = jnp.zeros_like(acc)
 
-    def fill(s, carry):
-        t, g = shifted(lax.rem(s * STEP, DEVICES))
-        gather(t * 4 + g, sbuf.at[s])
-
-        @pl.when(s > 1)
-        def _():
-            copy_of(s - 1).start()
-
-        return carry
+    def fill(step, last):
+        for i in range(4):
+            s = step * 4 + i
+            target = shifted(step, i)
+            gather(target[0] * 4 + target[1], sbuf.at[s])
+            if i < 2:
+
+                @pl.when(step > 0)
+                def _(s=s, last=last):
+                    copy_of(s - 1, last).start()
+
+            else:
+                copy_of(s - 1, last).start()
+            last = target
+        return last
 
     width = BATCH * PAD_ROWS
     high_id = lax.broadcasted_iota(I32, (FC, width), 0)
@@ -246,7 +275,7 @@
 
     def add_batch(b):
         def arrive(s, carry):
-            copy_of(s).wait_recv()
+            copy_of(s).wait()
             return carry
 
         lax.fori_loop(jnp.maximum(b * BATCH, 1), (b + 1) * BATCH, arrive, 0)
@@ -274,27 +303,29 @@
             )
         acc[...] = total
 
-    def stage(b, carry):
-        lax.fori_loop(jnp.maximum(b * BATCH, 1), (b + 1) * BATCH, fill, 0)
+    def stage(b, last):
+        last = lax.fori_loop(b * 4, b * 4 + 4, fill, last)
+
+        @pl.when(b == 0)
+        def _():
+            rbuf[0, 0:ROWS, :] = sbuf[0]
 
         @pl.when(b >= 2)
         def _():
             add_batch(b - 2)
 
-        return carry
-
-    lax.fori_loop(0, BATCHES, stage, 0)
-    copy_of(DEVICES - 1).start()
-    add_batch(BATCHES - 2)
-    add_batch(BATCHES - 1)
+        return last
+
+    last = lax.fori_loop(0, BATCHES, stage, (trial, geno))
+    copy_of(DEVICES - 1, last).start()
+
+    def tail(b, carry):
+        add_batch(b)
+        return carry
+
+    lax.fori_loop(BATCHES - 2, BATCHES, tail, 0)
     for q in range(4):
         out_ref[:, q * FC : (q + 1) * FC] = acc[q * 48 : (q + 1) * 48, :]
-
-    def sent(s, carry):
-        copy_of(s).wait_send()
-        return carry
-
-    lax.fori_loop(1, DEVICES, sent, 0)
 
 
 def body(probe_signs, trial_rows, trial_cols, ar_rho, res_var, plot_owner, plot_slot):
@@ -311,11 +342,11 @@
             pltpu.VMEM((FR + 2, PROBES, FC), F32),
             pltpu.VMEM((2, PROBES, FC), I32),
             pltpu.VMEM(((FR + 1) * FC, 128), I32),
-            pltpu.VMEM((DEVICES, FC), I32),
-            pltpu.SMEM((DEVICES, FC), I32),
+            pltpu.VMEM((SLOTS, DEVICES), I32),
+            pltpu.SMEM((SLOTS, DEVICES), I32),
             pltpu.VMEM((DEVICES, ROWS, 128), I32),
             pltpu.VMEM((DEVICES, PAD_ROWS, 128), I32),
-            pltpu.VMEM((DEVICES, 2 * SLOTS), F32),
+            pltpu.VMEM((SLOTS, 2 * DEVICES), F32),
             pltpu.VMEM((12 * PROBES, FC), F32),
             pltpu.SemaphoreType.DMA((PROBES,)),
             pltpu.SemaphoreType.DMA,
@@ -329,13 +360,13 @@
         ),
         name="hutchinson_exchange",
     )(
-        probe_signs.reshape(PROBES, FR, FC),
+        probe_signs.transpose(0, 1, 3, 2, 4).reshape(PROBES, FR, 1, FC),
         trial_rows,
         trial_cols,
         ar_rho,
         res_var,
-        plot_owner.reshape(FR, FC),
-        plot_slot.reshape(FR, FC),
+        plot_owner.transpose(0, 1, 2, 4, 3).reshape(FR, 1, FC),
+        plot_slot.transpose(0, 2, 1, 3).reshape(FR, 1, FC),
     )
     return out.reshape(3, PROBES, G_DEV)
 

time: 91.9 us -> 59.4 us (0.65)
  the two profiles are of different devices: /device:TPU:1 before, /device:TPU:24 now
where the time goes in v2:
time: 59.4 us; the launch traced here: 59.2 us
  Pallas kernels  55.6 us (94%)
  between operations  1.95 us (3%)
  local copies, waits for them, and re-layouts  1.62 us (3%)
    pallas_call x1, Pallas kernels, body(): pl.pallas_call(kernel, out_shape=jax.ShapeDtypeStruct((3 * PROBES, G_DEV)...  55.6 us
    unnamed x1, local copies, waits for them, and re-layouts  1.62 us

profile of v2, /device:TPU:24, one launch (start us, length us, event | category | flops | bytes accessed | tf_op | source)
XLA Modules:
  0.0 59.2 jit_solution(15684809053535298629)
XLA Ops:
  1.9 55.6 %hutchinson_exchange.1 = f32[48,1024]{1,0:T(8,128)} custom-call(s32[16,44,1,256]{3,2,1,0:T(1,128)} %bitcast.5, s32[1]{0:T(128)S(6)} %copy.9.rows_ref, s32[1]{0:T(128)S(6)} %copy.10.cols_ref, f32[1,2]{1,0:T(1,128)} %rho_ref.1, f32[1]{0:T(128)S(6)} %copy.11.var_ref, s32[44,1,256]{2,1,0:T(1,128)} %bitcast.6, s32[44,1,256]{2,1,0:T(1,128)} %bitcast.7), custom_call_target="tpu_custom_call" | custom-call | tf_op jit(solution)/shard_map/hutchinson_exchange/pallas_call | solution.py:334
  57.6 1.6 %copy.12 = f32[3,16,1024]{2,1,0:T(8,128)} copy(f32[3,16,1024]{2,1,0:T(8,128)} %bitcast.4) | data formatting | bytes 393216

commit v3 on v2

--- a/solution.py
+++ b/solution.py
@@ -17,8 +17,8 @@
 PAD_ROWS = 40
 BATCH = 16
 BATCHES = DEVICES // BATCH
-RANK_ROWS = 4
-TERM_ROWS = 3
+RANK_ROWS = 22
+TERM_ROWS = 7
 SCALE_BITS = 24
 MESH = pl.DeviceIdType.MESH
 F32 = jnp.float32
@@ -43,7 +43,7 @@
 
 def kernel(
     signs_ref, rows_ref, cols_ref, rho_ref, var_ref, owner_ref, slot_ref, out_ref,
-    xs, us, vs, halo, table, picks, picks_s, sbuf, rbuf, digits, acc,
+    owners, slots, xs, us, vs, halo, table, picks, picks_s, sbuf, rbuf, digits, acc,
     in_sem, pick_sem, halo_send, halo_recv, send_sem, recv_sem,
 ):
     trial, geno = lax.axis_index("trial"), lax.axis_index("geno")
@@ -53,7 +53,9 @@
         pltpu.make_async_copy(signs_ref.at[p, :, 0], xs.at[:, p, :], in_sem.at[p])
         for p in range(PROBES)
     ]
-    for load in loads:
+    owner_load = pltpu.make_async_copy(owner_ref, owners, in_sem.at[PROBES])
+    slot_load = pltpu.make_async_copy(slot_ref, slots, in_sem.at[PROBES + 1])
+    for load in [owner_load, *loads, slot_load]:
         load.start()
 
     def signal(step, i):
@@ -68,29 +70,41 @@
         signal(0, i)
     lax.fori_loop(1, DEVICES // 4, greet, 0)
 
-    owner_id = lax.broadcasted_iota(I32, (DEVICES, FC), 0)
+    def tall(row, height):
+        row = jnp.broadcast_to(row, (16, row.shape[1])).astype(F32).astype(BF16)
+        return jnp.concatenate([row] * (height // 16), axis=0)
+
+    def ids(height, width):
+        return lax.broadcasted_iota(I32, (height, width), 0).astype(F32).astype(BF16)
+
+    one, none = BF16(1), BF16(0)
+    owner_id = ids(DEVICES, FC)
+    place_id = ids(SLOTS, FC)
     col_i = lax.broadcasted_iota(I32, (FC, FC), 0)
     col_j = lax.broadcasted_iota(I32, (FC, FC), 1)
     upto = jnp.where(col_i <= col_j, F32(1), F32(0)).astype(BF16)
-    place_id = lax.broadcasted_iota(I32, (SLOTS, FC), 0)
-    col_f = lax.broadcasted_iota(I32, (1, FC), 1).astype(F32)
+    col_no = tall(lax.broadcasted_iota(I32, (1, FC), 1), DEVICES)
     digits[...] = jnp.zeros_like(digits)
+    owner_load.wait()
 
     def rank_rows(q, running):
+        owns = [owner_id == tall(owners[q * RANK_ROWS + i], DEVICES) for i in range(RANK_ROWS)]
+        hots = jnp.concatenate([jnp.where(own, one, none) for own in owns], axis=0)
+        counts = jnp.dot(hots, upto, preferred_element_type=F32)
         lefts, rights = [], []
-        for i in range(RANK_ROWS):
-            r = q * RANK_ROWS + i
-            own = owner_id == owner_ref[r]
-            hot = jnp.where(own, F32(1), F32(0)).astype(BF16)
-            count = jnp.dot(hot, upto, preferred_element_type=F32) + running
-            running = jnp.broadcast_to(count[:, FC - 1 :], (DEVICES, FC))
-            place = jnp.sum(jnp.where(own, count, F32(0)), axis=0, keepdims=True) - 1.0
-            lefts.append(jnp.where(place_id == place.astype(I32), F32(1), F32(0)).astype(BF16))
-            row_no = (r + 1).astype(F32)
+        for i, own in enumerate(owns):
+            count = counts[i * DEVICES : (i + 1) * DEVICES]
+            before = jnp.concatenate([running.astype(BF16)] * 2, axis=1)
+            running = running + jnp.broadcast_to(count[:, FC - 1 :], (DEVICES, 128))
+            mine = jnp.where(own, count.astype(BF16) + before, none)
+            parts = [mine[j * 16 : (j + 1) * 16] for j in range(DEVICES // 16)]
+            while len(parts) > 1:
+                parts = [x + y for x, y in zip(parts[::2], parts[1::2])]
+            place = jnp.sum(parts[0].astype(F32), axis=0, keepdims=True) - 1.0
+            lefts.append(jnp.where(place_id == tall(place, SLOTS), one, none))
+            row_no = tall(jnp.full((1, FC), q * RANK_ROWS + i + 1, I32), DEVICES)
             rights.append(
-                jnp.concatenate(
-                    [jnp.where(own, row_no, F32(0)), jnp.where(own, col_f, F32(0))], axis=0
-                ).astype(BF16)
+                jnp.concatenate([jnp.where(own, row_no, none), jnp.where(own, col_no, none)], axis=0)
             )
         digits[...] += lax.dot_general(
             jnp.concatenate(lefts, axis=1), jnp.concatenate(rights, axis=1),
@@ -98,7 +112,7 @@
         )
         return running
 
-    lax.fori_loop(0, FR // RANK_ROWS, rank_rows, jnp.zeros((DEVICES, FC), F32))
+    lax.fori_loop(0, FR // RANK_ROWS, rank_rows, jnp.zeros((DEVICES, 128), F32))
     plot = (digits[:, :DEVICES] * float(FC) + digits[:, DEVICES:]).astype(I32)
     picks[...] = jnp.clip(plot, 0, (FR + 1) * FC - 1)
     to_smem = pltpu.make_async_copy(picks, picks_s, pick_sem)
@@ -152,7 +166,7 @@
     )
     table[0:8, :] = jnp.where(lane8 >= 125, first_scales, jnp.where(lane8 >= 120, -1, 0))
 
-    for load in loads:
+    for load in [*loads, slot_load]:
         load.wait()
 
     def columns(bits, row):
@@ -208,7 +222,7 @@
         for value in values:
             q = jnp.floor(value + 0.5).astype(I32)
             words.append((q[8:] << 16) | (q[:8] & 0xFFFF))
-        aux = jnp.where(sub8 < PER_ROW, slot_ref[r], scale_rows)
+        aux = jnp.where(sub8 < PER_ROW, slots[r], scale_rows)
         stacked = jnp.concatenate(words * PER_ROW + [aux], axis=0)
         table[pl.ds(pl.multiple_of((r + 1) * FC, FC), FC), :] = stacked.T
 
@@ -270,7 +284,7 @@
         return last
 
     width = BATCH * PAD_ROWS
-    high_id = lax.broadcasted_iota(I32, (FC, width), 0)
+    high_id = ids(FC, width)
     pos = lax.rem(lax.broadcasted_iota(I32, (1, width), 1), PAD_ROWS)
 
     def add_batch(b):
@@ -284,24 +298,25 @@
             block[125 + t : 126 + t, :].astype(F32) * (1.0 / (float(1 << SCALE_BITS) * 32766.0))
             for t in range(3)
         ]
-        total = acc[...]
+        splits, hots = [], []
         for j in range(PER_ROW):
             slot = jnp.where(pos < ROWS, block[120 + j : 121 + j, :], -1)
             low = slot >> 8
-            hot = jnp.where(high_id == (slot & 255), F32(1), F32(0)).astype(BF16)
+            hots.append(jnp.where(high_id == tall(slot & 255, FC), one, none))
             parts = []
             for t in range(3):
                 word = block[(j * 3 + t) * 8 : (j * 3 + t + 1) * 8, :]
                 parts.append(((word << 16) >> 16).astype(F32) * scales[t])
                 parts.append((word >> 16).astype(F32) * scales[t])
-            values = jnp.concatenate(parts, axis=0)
-            split = jnp.concatenate(
-                [jnp.where(low == q, values, F32(0)) for q in range(4)], axis=0
-            ).astype(BF16)
-            total = total + lax.dot_general(
-                split, hot, (((1,), (1,)), ((), ())), preferred_element_type=F32
+            values = jnp.concatenate(parts, axis=0).astype(BF16)
+            low = tall(low, 48)
+            splits.append(
+                jnp.concatenate([jnp.where(low == BF16(q), values, none) for q in range(4)], axis=0)
             )
-        acc[...] = total
+        acc[...] += lax.dot_general(
+            jnp.concatenate(splits, axis=1), jnp.concatenate(hots, axis=1),
+            (((1,), (1,)), ((), ())), preferred_element_type=F32,
+        )
 
     def stage(b, last):
         last = lax.fori_loop(b * 4, b * 4 + 4, fill, last)
@@ -331,12 +346,15 @@
 def body(probe_signs, trial_rows, trial_cols, ar_rho, res_var, plot_owner, plot_slot):
     smem = pl.BlockSpec(memory_space=pltpu.SMEM)
     vmem = pl.BlockSpec(memory_space=pltpu.VMEM)
+    hbm = pl.BlockSpec(memory_space=pl.ANY)
     out = pl.pallas_call(
         kernel,
         out_shape=jax.ShapeDtypeStruct((3 * PROBES, G_DEV), F32),
-        in_specs=[pl.BlockSpec(memory_space=pl.ANY), smem, smem, smem, smem, vmem, vmem],
+        in_specs=[hbm, smem, smem, smem, smem, hbm, hbm],
         out_specs=vmem,
         scratch_shapes=[
+            pltpu.VMEM((FR, 1, FC), I32),
+            pltpu.VMEM((FR, 1, FC), I32),
             pltpu.VMEM((FR, PROBES, FC), I32),
             pltpu.VMEM((FR + 2, PROBES, FC), F32),
             pltpu.VMEM((FR + 2, PROBES, FC), F32),
@@ -348,7 +366,7 @@
             pltpu.VMEM((DEVICES, PAD_ROWS, 128), I32),
             pltpu.VMEM((SLOTS, 2 * DEVICES), F32),
             pltpu.VMEM((12 * PROBES, FC), F32),
-            pltpu.SemaphoreType.DMA((PROBES,)),
+            pltpu.SemaphoreType.DMA((PROBES + 2,)),
             pltpu.SemaphoreType.DMA,
             pltpu.SemaphoreType.DMA((2,)),
             pltpu.SemaphoreType.DMA((2,)),

time: 59.4 us -> 53.5 us (0.901)
  the two profiles are of different devices: /device:TPU:24 before, /device:TPU:1 now
where the time goes in v3:
time: 53.5 us; the launch traced here: 53.3 us
  Pallas kernels  49.8 us (93%)
  between operations  1.95 us (4%)
  local copies, waits for them, and re-layouts  1.62 us (3%)
    pallas_call x1, Pallas kernels, body(): pl.pallas_call(kernel, out_shape=jax.ShapeDtypeStruct((3 * PROBES, G_DEV)...  49.8 us
    unnamed x1, local copies, waits for them, and re-layouts  1.62 us

profile of v3, /device:TPU:1, one launch (start us, length us, event | category | flops | bytes accessed | tf_op | source)
XLA Modules:
  0.0 53.3 jit_solution(9315397525107120514)
XLA Ops:
  1.9 49.8 %hutchinson_exchange.1 = f32[48,1024]{1,0:T(8,128)} custom-call(s32[16,44,1,256]{3,2,1,0:T(1,128)} %bitcast.5, s32[1]{0:T(128)S(6)} %copy.9.rows_ref, s32[1]{0:T(128)S(6)} %copy.10.cols_ref, f32[1,2]{1,0:T(1,128)} %rho_ref.1, f32[1]{0:T(128)S(6)} %copy.11.var_ref, s32[44,1,256]{2,1,0:T(1,128)} %bitcast.6, s32[44,1,256]{2,1,0:T(1,128)} %bitcast.7), custom_call_target="tpu_custom_call" | custom-call | tf_op jit(solution)/shard_map/hutchinson_exchange/pallas_call | solution.py:350
  51.7 1.6 %copy.12 = f32[3,16,1024]{2,1,0:T(8,128)} copy(f32[3,16,1024]{2,1,0:T(8,128)} %bitcast.4) | data formatting | bytes 393216

commit v4 on v3

--- a/solution.py
+++ b/solution.py
@@ -26,24 +26,15 @@
 I32 = jnp.int32
 
 
-def places():
-    trial, geno = lax.axis_index("trial"), lax.axis_index("geno")
-    return trial // 8, lax.rem(trial // 2, 4), lax.rem(trial, 2), geno
-
-
-def shifted(step, i):
-    z, y, core, x = places()
-    far = step // 4
-    near = lax.rem(step, 4)
-    tz = lax.rem(z + lax.rem(far, 4) + 2 * near + i, 4)
-    ty = lax.rem(y + near, 4)
-    tc = lax.rem(core + far // 4 + near + i // 2, 2)
-    return tz * 8 + ty * 2 + tc, lax.rem(x + i, 4)
+def send_order():
+    shifts = [(k % 4, k // 4 % 4, k // 16 % 4, k // 64) for k in range(1, DEVICES)]
+    mixed = [shifts[(i * 50 + 13) % (DEVICES - 1)] for i in range(DEVICES - 1)]
+    return sorted(mixed, key=lambda d: -sum(min(d[a], 4 - d[a]) for a in range(3)))
 
 
 def kernel(
     signs_ref, rows_ref, cols_ref, rho_ref, var_ref, owner_ref, slot_ref, out_ref,
-    owners, slots, xs, us, vs, halo, table, picks, picks_s, sbuf, rbuf, digits, acc,
+    trials, genos, owners, slots, xs, us, vs, halo, table, picks, picks_s, sbuf, rbuf, digits, acc,
     in_sem, pick_sem, halo_send, halo_recv, send_sem, recv_sem,
 ):
     trial, geno = lax.axis_index("trial"), lax.axis_index("geno")
@@ -58,17 +49,18 @@
     for load in [owner_load, *loads, slot_load]:
         load.start()
 
-    def signal(step, i):
-        pl.semaphore_signal(barrier, inc=1, device_id=shifted(step, i), device_id_type=MESH)
-
-    def greet(step, carry):
-        for i in range(4):
-            signal(step, i)
-        return carry
-
-    for i in range(1, 4):
-        signal(0, i)
-    lax.fori_loop(1, DEVICES // 4, greet, 0)
+    z, y, core = trial // 8, lax.rem(trial // 2, 4), lax.rem(trial, 2)
+    xs_at = [lax.rem(geno + i, 4) for i in range(4)]
+    ys_at = [lax.rem(y + i, 4) * 2 for i in range(4)]
+    zs_at = [lax.rem(z + i, 4) * 8 for i in range(4)]
+    cores_at = [core, 1 - core]
+    trials[0] = trial
+    genos[0] = geno
+    for s, (dx, dy, dz, dc) in enumerate(send_order(), 1):
+        t, g = zs_at[dz] + ys_at[dy] + cores_at[dc], xs_at[dx]
+        pl.semaphore_signal(barrier, inc=1, device_id=(t, g), device_id_type=MESH)
+        trials[s] = t
+        genos[s] = g
 
     def tall(row, height):
         row = jnp.broadcast_to(row, (16, row.shape[1])).astype(F32).astype(BF16)
@@ -270,7 +262,7 @@
     def fill(step, last):
         for i in range(4):
             s = step * 4 + i
-            target = shifted(step, i)
+            target = trials[s], genos[s]
             gather(target[0] * 4 + target[1], sbuf.at[s])
             if i < 2:
 
@@ -349,10 +341,12 @@
     hbm = pl.BlockSpec(memory_space=pl.ANY)
     out = pl.pallas_call(
         kernel,
-        out_shape=jax.ShapeDtypeStruct((3 * PROBES, G_DEV), F32),
+        out_shape=pltpu.VMEM((3 * PROBES, G_DEV), F32),
         in_specs=[hbm, smem, smem, smem, smem, hbm, hbm],
         out_specs=vmem,
         scratch_shapes=[
+            pltpu.SMEM((DEVICES,), I32),
+            pltpu.SMEM((DEVICES,), I32),
             pltpu.VMEM((FR, 1, FC), I32),
             pltpu.VMEM((FR, 1, FC), I32),
             pltpu.VMEM((FR, PROBES, FC), I32),

time: 53.5 us -> 53.5 us (level)
  local copies, waits for them, and re-layouts: 1.62 us -> 0.68 us
  Pallas kernels: 49.8 us -> 50.7 us
    unnamed x1, local copies, waits for them, and re-layouts: 1.62 us -> 0.68 us
    pallas_call x1, Pallas kernels: 49.8 us -> 50.7 us  [body(): pl.pallas_call(kernel, out_shape=pltpu.VMEM((3 * PROBES, G_DEV), F32), in...]
where the time goes in v4:
time: 53.5 us; the launch traced here: 53.3 us
  Pallas kernels  50.7 us (95%)
  between operations  1.95 us (4%)
  local copies, waits for them, and re-layouts  0.68 us (1%)
    pallas_call x1, Pallas kernels, body(): pl.pallas_call(kernel, out_shape=pltpu.VMEM((3 * PROBES, G_DEV), F32), in...  50.7 us

profile of v4, /device:TPU:1, one launch (start us, length us, event | category | flops | bytes accessed | tf_op | source)
XLA Modules:
  0.0 53.3 jit_solution(1753529187362220578)
XLA Ops:
  1.9 50.7 %hutchinson_exchange.1 = f32[48,1024]{1,0:T(8,128)S(1)} custom-call(s32[16,44,1,256]{3,2,1,0:T(1,128)} %bitcast.5, s32[1]{0:T(128)S(6)} %copy.10.rows_ref, s32[1]{0:T(128)S(6)} %copy.11.cols_ref, f32[1,2]{1,0:T(1,128)} %rho_ref.1, f32[1]{0:T(128)S(6)} %copy.12.var_ref, s32[44,1,256]{2,1,0:T(1,128)} %bitcast.6, s32[44,1,256]{2,1,0:T(1,128)} %bitcast.7), custom_call_target="tpu_custom_call" | custom-call | tf_op jit(solution)/shard_map/hutchinson_exchange/pallas_call | solution.py:342
  52.6 0.7 %copy.9 = f32[3,16,1024]{2,1,0:T(8,128)} copy(f32[3,16,1024]{2,1,0:T(8,128)S(1)} %bitcast.4) | data formatting | bytes 393216

commit v5 on v4

--- a/solution.py
+++ b/solution.py
@@ -27,9 +27,11 @@
 
 
 def send_order():
-    shifts = [(k % 4, k // 4 % 4, k // 16 % 4, k // 64) for k in range(1, DEVICES)]
-    mixed = [shifts[(i * 50 + 13) % (DEVICES - 1)] for i in range(DEVICES - 1)]
-    return sorted(mixed, key=lambda d: -sum(min(d[a], 4 - d[a]) for a in range(3)))
+    out = []
+    for s in range(1, DEVICES):
+        i, near, far = s % 4, s // 4 % 4, s // 16
+        out.append((i, near, (far + 2 * near + i) % 4, (far // 4 + near + i // 2) % 2))
+    return out
 
 
 def kernel(

time: 53.5 us -> 51.4 us (0.961)
  Pallas kernels: 50.7 us -> 48.5 us
    pallas_call x1, Pallas kernels: 50.7 us -> 48.5 us  [body(): pl.pallas_call(kernel, out_shape=pltpu.VMEM((3 * PROBES, G_DEV), F32), in...]
where the time goes in v5:
time: 51.4 us; the launch traced here: 51.1 us
  Pallas kernels  48.5 us (94%)
  between operations  1.95 us (4%)
  local copies, waits for them, and re-layouts  0.68 us (1%)
    pallas_call x1, Pallas kernels, body(): pl.pallas_call(kernel, out_shape=pltpu.VMEM((3 * PROBES, G_DEV), F32), in...  48.5 us

profile of v5, /device:TPU:1, one launch (start us, length us, event | category | flops | bytes accessed | tf_op | source)
XLA Modules:
  0.0 51.1 jit_solution(7461828835744816449)
XLA Ops:
  1.9 48.5 %hutchinson_exchange.1 = f32[48,1024]{1,0:T(8,128)S(1)} custom-call(s32[16,44,1,256]{3,2,1,0:T(1,128)} %bitcast.5, s32[1]{0:T(128)S(6)} %copy.10.rows_ref, s32[1]{0:T(128)S(6)} %copy.11.cols_ref, f32[1,2]{1,0:T(1,128)} %rho_ref.1, f32[1]{0:T(128)S(6)} %copy.12.var_ref, s32[44,1,256]{2,1,0:T(1,128)} %bitcast.6, s32[44,1,256]{2,1,0:T(1,128)} %bitcast.7), custom_call_target="tpu_custom_call" | custom-call | tf_op jit(solution)/shard_map/hutchinson_exchange/pallas_call | solution.py:344
  50.5 0.7 %copy.9 = f32[3,16,1024]{2,1,0:T(8,128)} copy(f32[3,16,1024]{2,1,0:T(8,128)S(1)} %bitcast.4) | data formatting | bytes 393216

commit v6 on v5

--- a/solution.py
+++ b/solution.py
@@ -30,7 +30,7 @@
     out = []
     for s in range(1, DEVICES):
         i, near, far = s % 4, s // 4 % 4, s // 16
-        out.append((i, near, (far + 2 * near + i) % 4, (far // 4 + near + i // 2) % 2))
+        out.append((near, i, (far + 2 * near + i) % 4, (far // 4 + near + i // 2) % 2))
     return out
 
 

time: 51.4 us -> 52.7 us (1.025)
  Pallas kernels: 48.5 us -> 49.5 us
    pallas_call x1, Pallas kernels: 48.5 us -> 49.5 us  [body(): pl.pallas_call(kernel, out_shape=pltpu.VMEM((3 * PROBES, G_DEV), F32), in...]
where the time goes in v6:
time: 52.7 us; the launch traced here: 52.1 us
  Pallas kernels  49.5 us (94%)
  between operations  1.95 us (4%)
  local copies, waits for them, and re-layouts  0.68 us (1%)
    pallas_call x1, Pallas kernels, body(): pl.pallas_call(kernel, out_shape=pltpu.VMEM((3 * PROBES, G_DEV), F32), in...  49.5 us

profile of v6, /device:TPU:1, one launch (start us, length us, event | category | flops | bytes accessed | tf_op | source)
XLA Modules:
  0.0 52.1 jit_solution(14828848168928254230)
XLA Ops:
  1.9 49.5 %hutchinson_exchange.1 = f32[48,1024]{1,0:T(8,128)S(1)} custom-call(s32[16,44,1,256]{3,2,1,0:T(1,128)} %bitcast.5, s32[1]{0:T(128)S(6)} %copy.10.rows_ref, s32[1]{0:T(128)S(6)} %copy.11.cols_ref, f32[1,2]{1,0:T(1,128)} %rho_ref.1, f32[1]{0:T(128)S(6)} %copy.12.var_ref, s32[44,1,256]{2,1,0:T(1,128)} %bitcast.6, s32[44,1,256]{2,1,0:T(1,128)} %bitcast.7), custom_call_target="tpu_custom_call" | custom-call | tf_op jit(solution)/shard_map/hutchinson_exchange/pallas_call | solution.py:344
  51.5 0.7 %copy.9 = f32[3,16,1024]{2,1,0:T(8,128)} copy(f32[3,16,1024]{2,1,0:T(8,128)S(1)} %bitcast.4) | data formatting | bytes 393216
